TPU v7x, 32 devices: a whole 2x2x4 slice. The times are simulated.
32 devices in a mesh: chan: 4 (over z), pulse: 4 (over x, core), range: 2 (over y).
Axes of the slice: x: 2, y: 2, z: 4, core: 2. Of those that a mesh axis runs over, the one named last changes fastest.
Arguments:
- signal: bfloat16 [2, 64, 32, 8192], P(None, 'chan', 'pulse', 'range'), may hold values from -6 to 6
- steering: bfloat16 [2, 32, 64], replicated, may hold values from -0.5 to 0.5
- spectrum: float32 [2, 8192], replicated, may hold values from -6 to 6
Outputs:
- detection: float32 [32, 32, 8192], P('chan', 'pulse', 'range')
All inputs are finite; a program needn't handle non-finite values.
Results may differ from a plain program's by a relative error of at most 0.0087.
Values may be sent and summed in bfloat16 or wider, within the bound.
A program may use at most 64 MiB of HBM per device.

v0:
```python
import math
import jax
import jax.numpy as jnp
from jax import lax
from jax.sharding import PartitionSpec as P

GUARD = 4
TRAIN = 16
PRECISE = lax.Precision.HIGHEST
NOISE_FLOOR = 0.25


def padded_2(x, sides, width):
    for axis, dim in sides:
        peers, length = (lax.axis_size(axis), x.shape[dim])
        up = [(i, (i + 1) % peers) for i in range(peers - 1)]
        down = [(j, i) for i, j in up]
        last = lax.slice_in_dim(x, length - width, length, axis=dim)
        initial = lax.slice_in_dim(x, 0, width, axis=dim)
        before = lax.ppermute(last, axis, up)
        after = lax.ppermute(initial, axis, down)
        x = jnp.concatenate([before, x, after], axis=dim)
    return x


def doppler_tables(pulse_count):
    row_ids = lax.broadcasted_iota(jnp.int32, (pulse_count, pulse_count), 0)
    col_ids = lax.broadcasted_iota(jnp.int32, (pulse_count, pulse_count), 1)
    phase_angle = (row_ids * col_ids % pulse_count).astype(jnp.float32) * (
        2.0 * math.pi / pulse_count
    )
    norm_scale = 1.0 / math.sqrt(pulse_count)
    table_real = (jnp.cos(phase_angle) * norm_scale).astype(jnp.bfloat16)
    table_imag = (-jnp.sin(phase_angle) * norm_scale).astype(jnp.bfloat16)
    return (table_real, table_imag)


def phase_table(row_count, col_count, period_len, direction):
    row_ids = lax.broadcasted_iota(jnp.int32, (row_count, col_count), 0)
    col_ids = lax.broadcasted_iota(jnp.int32, (row_count, col_count), 1)
    phase_angle = (row_ids * col_ids % period_len).astype(jnp.float32) * (
        2.0 * math.pi / period_len
    )
    return (jnp.cos(phase_angle), direction * jnp.sin(phase_angle))


def rotate_by(field_pair, table_pair):
    return (
        field_pair[0] * table_pair[0] - field_pair[1] * table_pair[1],
        field_pair[0] * table_pair[1] + field_pair[1] * table_pair[0],
    )


def mix_blocks(table_pair, field_pair):

    def contract(table_part, field_part):
        return jnp.einsum("km,bpmn->bpkn", table_part, field_part, precision=PRECISE)

    return (
        contract(table_pair[0], field_pair[0]) - contract(table_pair[1], field_pair[1]),
        contract(table_pair[0], field_pair[1]) + contract(table_pair[1], field_pair[0]),
    )


def mix_lanes(field_pair, table_pair):

    def contract(field_part, table_part):
        return jnp.einsum("bpkm,mn->bpkn", field_part, table_part, precision=PRECISE)

    return (
        contract(field_pair[0], table_pair[0]) - contract(field_pair[1], table_pair[1]),
        contract(field_pair[0], table_pair[1]) + contract(field_pair[1], table_pair[0]),
    )


def local_transform(field_pair, direction):
    size_all = field_pair[0].shape[-1]
    blocks = size_all // 128
    leading = field_pair[0].shape[:-1]
    shaped = tuple((member.reshape(leading + (blocks, 128)) for member in field_pair))
    outer_table = phase_table(blocks, blocks, blocks, direction)
    twiddle = phase_table(blocks, 128, size_all, direction)
    inner_table = phase_table(128, 128, 128, direction)
    if direction < 0:
        shaped = mix_blocks(outer_table, shaped)
        shaped = rotate_by(shaped, twiddle)
        shaped = mix_lanes(shaped, inner_table)
    else:
        shaped = mix_lanes(shaped, inner_table)
        shaped = rotate_by(shaped, twiddle)
        shaped = mix_blocks(outer_table, shaped)
    return tuple((member.reshape(leading + (size_all,)) for member in shaped))


def stack_weights(w_real, w_imag):
    return jnp.concatenate(
        [jnp.concatenate([w_real, -w_imag], 1), jnp.concatenate([w_imag, w_real], 1)], 0
    )


def shards(signal, steering, spectrum):
    beam_count = steering.shape[1]
    chan_count = steering.shape[2]
    pulse_local = signal.shape[2]
    gate_count = signal.shape[3]
    stacked = stack_weights(steering[0], steering[1])
    samples = lax.all_to_all(signal, "chan", split_axis=2, concat_axis=1, tiled=True)
    pulses_here = samples.shape[2]
    gates_here = samples.shape[3]
    flat_samples = samples.reshape(2 * chan_count, pulses_here * gates_here)
    formed = jnp.dot(stacked, flat_samples, preferred_element_type=jnp.float32)
    formed = formed.astype(jnp.bfloat16).reshape(2, beam_count, pulses_here, gates_here)
    beam_data = lax.all_to_all(formed, "chan", split_axis=1, concat_axis=2, tiled=True)
    beam_local = beam_data.shape[1]
    range_count = lax.axis_size("range")
    range_index = lax.axis_index("range")
    full_length = gate_count * range_count
    inverse_scale = 1.0 / full_length
    shard_piece = lax.all_gather(beam_data, "range", axis=3, tiled=True)
    shard_count = shard_piece.shape[3] // gate_count
    members = shard_piece.astype(jnp.float32).reshape(
        2, beam_local, pulse_local, shard_count, gate_count
    )
    source = jnp.arange(shard_count, dtype=jnp.int32)
    phase_angle = (source * range_index % range_count).astype(jnp.float32) * (
        2.0 * math.pi / range_count
    )
    cos_part = jnp.cos(phase_angle)[:, None]
    sin_part = -jnp.sin(phase_angle)[:, None]
    sum_real = jnp.sum(members[0] * cos_part - members[1] * sin_part, axis=2)
    sum_imag = jnp.sum(members[0] * sin_part + members[1] * cos_part, axis=2)
    folded = (sum_real, sum_imag)
    gate_ids = lax.broadcasted_iota(jnp.int32, (gate_count,), 0)
    global_angle = (gate_ids * range_index % full_length).astype(jnp.float32) * (
        2.0 * math.pi / full_length
    )
    folded = rotate_by(folded, (jnp.cos(global_angle), -jnp.sin(global_angle)))
    spectrum_local = local_transform(folded, -1.0)
    response = spectrum.reshape(2, gate_count, range_count)
    response = lax.dynamic_index_in_dim(response, range_index, axis=2, keepdims=False)
    response = jnp.transpose(response.reshape(2, 128, gate_count // 128), (0, 2, 1)).reshape(
        2, gate_count
    )
    filtered = rotate_by(spectrum_local, (response[0], response[1]))
    restored = local_transform(filtered, 1.0)
    restored = rotate_by(restored, (jnp.cos(global_angle), jnp.sin(global_angle)))
    shard_piece = (
        lax.all_gather(restored[0], "range", axis=2, tiled=True),
        lax.all_gather(restored[1], "range", axis=2, tiled=True),
    )
    shard_count = shard_piece[0].shape[2] // gate_count
    rows_real = shard_piece[0].reshape(beam_local, pulse_local, shard_count, gate_count)
    rows_imag = shard_piece[1].reshape(beam_local, pulse_local, shard_count, gate_count)
    source = jnp.arange(shard_count, dtype=jnp.int32)
    phase_angle = (source * range_index % range_count).astype(jnp.float32) * (
        2.0 * math.pi / range_count
    )
    cos_part = jnp.cos(phase_angle)[:, None]
    sin_part = jnp.sin(phase_angle)[:, None]
    sum_real = jnp.sum(rows_real * cos_part - rows_imag * sin_part, axis=2)
    sum_imag = jnp.sum(rows_real * sin_part + rows_imag * cos_part, axis=2)
    compressed = jnp.stack([sum_real * inverse_scale, sum_imag * inverse_scale]).astype(
        jnp.bfloat16
    )
    pulse_total = pulse_local * lax.axis_size("pulse")
    dop_real, dop_imag = doppler_tables(pulse_total)
    columns = lax.all_to_all(compressed, "pulse", split_axis=3, concat_axis=2, tiled=True)

    def product(table_part, values):
        return jnp.einsum("fp,bpr->bfr", table_part, values, preferred_element_type=jnp.float32)

    mixed_real = product(dop_real, columns[0]) - product(dop_imag, columns[1])
    mixed_imag = product(dop_real, columns[1]) + product(dop_imag, columns[0])
    power_part = lax.all_to_all(
        mixed_real * mixed_real + mixed_imag * mixed_imag,
        "pulse",
        split_axis=1,
        concat_axis=2,
        tiled=True,
    )
    halo_width = GUARD + TRAIN
    padded = padded_2(power_part, (("range", 2),), halo_width)
    window_sum = jnp.zeros_like(power_part)
    for offset in range(1, TRAIN + 1):
        left_start = halo_width - GUARD - offset
        right_start = halo_width + GUARD + offset
        window_sum = (
            window_sum
            + padded[:, :, left_start : left_start + gate_count]
            + padded[:, :, right_start : right_start + gate_count]
        )
    noise_level = window_sum / (2.0 * TRAIN)
    return power_part / (noise_level + NOISE_FLOOR)


def solution(mesh):
    in_specs = (P(None, "chan", "pulse", "range"), P(), P())
    out_specs = P("chan", "pulse", "range")
    return jax.shard_map(shards, mesh=mesh, in_specs=in_specs, out_specs=out_specs, check_vma=False)
```

profile of v0, /device:TPU:0, one launch (start us, length us, event | category | flops | bytes accessed | tf_op | source)
XLA Modules:
  0.0 388.4 jit_solution(4963313028370823325)
XLA Ops:
  6.5 4.1 %copy.81 = bf16[2,16,8,4096]{3,1,0,2:T(8,128)(2,1)} copy(bf16[2,16,8,4096]{3,2,1,0:T(8,128)(2,1)} %param.3) | data formatting | bytes 4194304 | tf_op args[0]
  10.6 6.5 %all-to-all-start = ((bf16[2,16,8,4096]{3,1,0,2:T(8,128)(2,1)}), bf16[2,16,8,4096]{3,1,0,2:T(8,128)(2,1)S(1)}, u32[]{:S(2)}, u32[]{:S(2)}) async-start(bf16[2,16,8,4096]{3,1,0,2:T(8,128)(2,1)} %copy.81), calls=%async_computation | async-start | bytes 4194304 | tf_op jit(solution)/shard_map/all_to_all | solution.py:107
  17.1 48.2 %all-to-all-done = bf16[2,16,8,4096]{3,1,0,2:T(8,128)(2,1)S(1)} async-done(((bf16[2,16,8,4096]{3,1,0,2:T(8,128)(2,1)}), bf16[2,16,8,4096]{3,1,0,2:T(8,128)(2,1)S(1)}, u32[]{:S(2)}, u32[]{:S(2)}) %all-to-all-start) | async-done | bytes 2097184 | tf_op jit(solution)/shard_map/all_to_all | solution.py:107
  65.3 2.2 copy.82
  67.5 1.3 copy.126
  69.3 0.8 reshape.187
  70.1 0.9 copy.83
  71.0 27.7 %all_to_all.66 = bf16[2,32,2,4096]{3,2,0,1:T(2,128)(2,1)S(1)} all-to-all(bf16[2,32,2,4096]{3,2,0,1:T(2,128)(2,1)S(1)} %copy.83), channel_id=1, replica_groups=mesh['chan'=4,'pulse'=4,'range'=2] {'chan'}, dimensions={1} | all-to-all | bytes 2097152 | tf_op jit(solution)/shard_map/all_to_all | solution.py:113
  99.3 1.0 copy.85
  100.6 6.4 %reshape.188 = f32[2,4096,2]{2,1,0:T(8,128)} reshape(f32[2,8192]{1,0:T(2,128)S(1)} %copy-done.1) | data formatting | bytes 131072 | tf_op jit(solution)/shard_map/reshape | solution.py:139
  107.0 4.7 %dynamic-slice_reduce_fusion = f32[2,4096]{1,0:T(2,128)S(1)} fusion(f32[2,4096,2]{2,1,0:T(8,128)} %reshape.188, s32[]{:T(128)S(6)} %select_n.134), kind=kLoop, calls=%fused_computation.31 | loop fusion | bytes 65540 | tf_op jit(solution)/shard_map/jit(dynamic_index_in_dim)/dynamic_slice | solution.py:140
  112.5 20.2 %all-gather.4.cloned.1.call-done = bf16[2,8,8,8192]{3,1,2,0:T(8,128)(2,1)} async-done(((bf16[2,8,8,4096]{3,1,2,0:T(8,128)(2,1)}), bf16[2,8,8,8192]{3,1,2,0:T(8,128)(2,1)}) %all-gather.4.cloned.1.call-update) | async-done | bytes 2097168 | tf_op jit(solution)/shard_map/all_gather | solution.py:119
  132.7 3.9 %fusion.271 = (f32[1,8,8,8192]{3,1,2,0:T(8,128)}, f32[1,8,8,8192]{3,1,2,0:T(8,128)}) fusion(bf16[2,8,8,8192]{3,1,2,0:T(8,128)(2,1)} %all-gather.4.cloned.1.call-done), kind=kLoop, calls=%fused_computation.365 | loop fusion | bytes 8388608 | tf_op jit(solution)/shard_map/slice | solution.py:130
  136.6 3.0 reshape.202
  139.7 4.4 %reshape.203 = f32[8,8,2,4096]{3,2,0,1:T(2,128)} reshape(f32[1,8,8,8192]{3,1,2,0:T(8,128)} %get-tuple-element.12) | data formatting | bytes 4194304 | tf_op jit(solution)/shard_map/squeeze | solution.py:130
  144.1 5.8 %subtract_reduce_fusion.1 = (f32[8,8,4096]{2,1,0:T(8,128)S(1)}, f32[8,8,4096]{2,1,0:T(8,128)S(1)}) fusion(f32[8,8,2,4096]{3,2,0,1:T(2,128)} %reshape.203, f32[8,8,2,4096]{3,2,0,1:T(2,128)S(1)} %reshape.202, f32[2]{0:T(128)S(1)} %get-tuple-element.24, f32[2]{0:T(128)S(1)} %get-tuple-element.23), kind=kLoop, calls=%fused_computation.35 | loop fusion | flops 3670016 | bytes 6291472 | tf_op jit(solution)/shard_map/reduce_sum | solution.py:130
  151.1 1.5 fusion.85
  152.6 1.5 fusion.84
  154.1 1.5 fusion.2
  155.6 1.5 fusion.3
  157.1 1.4 fusion.78
  158.5 1.2 fusion.79
  159.8 1.2 convolution_add_fusion.2
  161.0 1.2 convolution_subtract_fusion.2
  162.2 1.2 fusion.80
  163.5 1.2 fusion.81
  164.7 1.2 convolution_add_fusion.1
  165.9 1.2 convolution_subtract_fusion.1
  167.2 1.2 fusion.83
  168.4 1.4 fusion.82
  169.8 2.2 fusion
  172.0 2.4 reshape.191
  174.3 2.2 fusion.1
  176.5 1.5 reshape.190
  178.1 1.6 multiply_subtract_fusion
  180.4 32.5 %all-gather.6.cloned.1.call-done = f32[8,8,8192]{2,1,0:T(8,128)} async-done(((f32[8,8,4096]{2,1,0:T(8,128)}), f32[8,8,8192]{2,1,0:T(8,128)}) %all-gather.6.cloned.1.call-update) | async-done | bytes 2097168 | tf_op jit(solution)/shard_map/all_gather | solution.py:148
  212.9 34.7 %all-gather.8.cloned.1.call-done = f32[8,8,8192]{2,1,0:T(8,128)} async-done(((f32[8,8,4096]{2,1,0:T(8,128)}), f32[8,8,8192]{2,1,0:T(8,128)}) %all-gather.8.cloned.1.call-update) | async-done | bytes 2097168 | tf_op jit(solution)/shard_map/all_gather | solution.py:149
  247.6 3.2 subtract_reduce_fusion
  252.1 14.0 %copy.106 = bf16[2,8,8,4096]{2,1,0,3:T(8,128)(2,1)} copy(bf16[2,8,8,4096]{3,1,2,0:T(8,128)(2,1)S(1)} %pad_maximum_fusion.2) | data formatting | bytes 2097152 | tf_op jit(solution)/shard_map/stack | solution.py:162
  266.1 20.5 %reshape.205 = bf16[4,2,65536]{2,1,0:T(2,128)(2,1)S(1)} reshape(bf16[4096,2,8,8]{3,2,1,0:T(8,128)(2,1)} %bitcast.133) | data formatting | bytes 2097152
  286.6 17.2 %all_to_all.67 = bf16[4,2,65536]{2,1,0:T(2,128)(2,1)S(1)} all-to-all(bf16[4,2,65536]{2,1,0:T(2,128)(2,1)S(1)} %reshape.205), channel_id=1, replica_groups=mesh['chan'=4,'pulse'=4,'range'=2] {'pulse'}, dimensions={0} | all-to-all | bytes 2097152 | tf_op jit(solution)/shard_map/all_to_all | solution.py:167
  303.8 21.7 %reshape.206 = bf16[4096,2,8,8]{3,2,1,0:T(8,128)(2,1)} reshape(bf16[4,2,65536]{2,1,0:T(2,128)(2,1)S(1)} %all_to_all.67) | data formatting | bytes 2097152
  325.5 16.0 %copy.107 = bf16[2,8,8,4,1024]{4,2,3,1,0:T(8,128)(2,1)S(1)} copy(bf16[2,8,8,4,1024]{2,1,0,4,3:T(8,128)(2,1)} %bitcast.134) | data formatting | bytes 2097152 | tf_op jit(solution)/shard_map/all_to_all | solution.py:167
  343.6 16.9 %all_to_all.68 = f32[8,32,1024]{2,0,1:T(8,128)S(1)} all-to-all(f32[8,32,1024]{2,0,1:T(8,128)S(1)} %copy.108), channel_id=1, replica_groups=mesh['chan'=4,'pulse'=4,'range'=2] {'pulse'}, dimensions={1} | all-to-all | bytes 2097152 | tf_op jit(solution)/shard_map/all_to_all | solution.py:174
  361.2 2.4 collective-permute-start
  363.6 1.3 collective-permute-start.1
  365.2 4.2 %collective-permute-done.1 = f32[8,8,20]{2,1,0:T(8,128)S(1)} collective-permute-done((f32[8,8,20]{2,1,0:T(8,128)S(1)}, f32[8,8,20]{2,1,0:T(8,128)S(1)}, u32[]{:S(2)}, u32[]{:S(2)}) %collective-permute-start.1) | collective-permute-done | bytes 5152 | tf_op jit(solution)/shard_map/ppermute | solution.py:21
  369.4 12.0 %fusion.14 = f32[8,8,4096]{2,1,0:T(8,128)} fusion(f32[8,8,4096]{2,1,0:T(8,128)S(1)} %bitcast.151, f32[8,8,20]{2,1,0:T(8,128)S(1)} %collective-permute-done.1, f32[8,8,20]{2,1,0:T(8,128)S(1)} %collective-permute-done), kind=kLoop, calls=%fused_computation.60 | loop fusion | flops 17301504 | bytes 2107392 | tf_op jit(solution)/shard_map/div | solution.py:193
  (39 shorter events, 8.4 us)
Async XLA Ops:
  10.6 6.5 %copy-start.2 = (bf16[2,32,64]{2,1,0:T(8,128)(2,1)S(1)}, bf16[2,32,64]{2,1,0:T(8,128)(2,1)}, u32[]{:S(2)}) copy-start(bf16[2,32,64]{2,1,0:T(8,128)(2,1)} %param.4) | copy-start | bytes 24580
  10.6 54.7 %all-to-all-start = ((bf16[2,16,8,4096]{3,1,0,2:T(8,128)(2,1)}), bf16[2,16,8,4096]{3,1,0,2:T(8,128)(2,1)S(1)}, u32[]{:S(2)}, u32[]{:S(2)}) async-start(bf16[2,16,8,4096]{3,1,0,2:T(8,128)(2,1)} %copy.81), calls=%async_computation | async-start | bytes 4194304 | tf_op jit(solution)/shard_map/all_to_all | solution.py:107
  17.1 115.6 %all-gather.4.cloned.1.call-start = ((), (), s32[]{:S(2)}) async-start(), calls=%async_computation.4 | async-start | bytes 3145728 | tf_op jit(solution)/shard_map/all_gather | solution.py:119
  99.3 1.3 copy-start.1
  100.4 112.5 %all-gather.6.cloned.1.call-start = ((), (), s32[]{:S(2)}) async-start(), calls=%async_computation.5 | async-start | bytes 3145728 | tf_op jit(solution)/shard_map/all_gather | solution.py:148
  176.5 1.5 copy-start
  179.7 67.9 %all-gather.8.cloned.1.call-start = ((), (), s32[]{:S(2)}) async-start(), calls=%async_computation.6 | async-start | bytes 3145728 | tf_op jit(solution)/shard_map/all_gather | solution.py:149
  361.2 4.0 %collective-permute-start = (f32[8,8,20]{2,1,0:T(8,128)S(1)}, f32[8,8,20]{2,1,0:T(8,128)S(1)}, u32[]{:S(2)}, u32[]{:S(2)}) collective-permute-start(f32[8,8,20]{2,1,0:T(8,128)S(1)} %get-tuple-element.13), channel_id=1, source_target_pairs={{0,1},{2,3},{4,5},{6,7},{8,9},{10,11},{12,13},{14,15},{16,17},{18,... | collective-permute-start | bytes 15368 | tf_op jit(solution)/shard_map/ppermute | solution.py:20
  363.6 5.8 %collective-permute-start.1 = (f32[8,8,20]{2,1,0:T(8,128)S(1)}, f32[8,8,20]{2,1,0:T(8,128)S(1)}, u32[]{:S(2)}, u32[]{:S(2)}) collective-permute-start(f32[8,8,20]{2,1,0:T(8,128)S(1)} %get-tuple-element.14), channel_id=1, source_target_pairs={{1,0},{3,2},{5,4},{7,6},{9,8},{11,10},{13,12},{15,14},{17,16},{19,... | collective-permute-start | bytes 15368 | tf_op jit(solution)/shard_map/ppermute | solution.py:21
Sparse Core Ops, SparseCore 0:
  100.5 32.1 all-gather.3
  179.8 33.0 all-gather.5
  214.5 33.0 all-gather.7
where the time goes:
time: 395 us; the launch traced here: 388 us
  waiting for transfers between devices  141 us (36%)
  local copies, waits for them, and re-layouts  112 us (28%)
  blocking collectives  61.8 us (16%)
  matrix products  24.9 us (6%)
  other arithmetic  24.3 us (6%)
  between operations  13.9 us (4%)
  starting transfers between devices  10.5 us (3%)
    unnamed x12, local copies, waits for them, and re-layouts  48.9 us
    all_to_all x1, waiting for transfers between devices, shards(): lax.all_to_all(signal, 'chan', split_axis=2, concat_axis=1, tiled=True)  48.2 us
    all_gather x1, waiting for transfers between devices, shards(): lax.all_gather(restored[1], 'range', axis=2, tiled=True)  34.7 us
    all_gather x1, waiting for transfers between devices, shards(): lax.all_gather(restored[0], 'range', axis=2, tiled=True)  32.5 us
    all_to_all x1, blocking collectives, shards(): lax.all_to_all(formed, 'chan', split_axis=1, concat_axis=2, tiled=True)  27.7 us
    all_gather x1, waiting for transfers between devices, shards(): shard_piece = lax.all_gather(beam_data, 'range', axis=3, tiled=True)  20.2 us
    all_to_all x1, blocking collectives, shards(): lax.all_to_all(compressed, 'pulse', split_axis=3, concat_axis=2, tiled=True)  17.2 us
    all_to_all x1, blocking collectives, shards(): lax.all_to_all(mixed_real * mixed_real + mixed_imag * mixed_imag, 'pulse'...  16.9 us
  transfers between devices with their start and end apart: 6, of which 6 were waited for; matrix products, arithmetic and copies ran while one was open for 3% of the time, Pallas kernels for 0%

commit v1 on v0

--- a/solution.py
+++ b/solution.py
@@ -8,6 +8,18 @@
 TRAIN = 16
 PRECISE = lax.Precision.HIGHEST
 NOISE_FLOOR = 0.25
+
+
+def gather_by_bits(array, axis, dim):
+    ways, here, hop = (lax.axis_size(axis), lax.axis_index(axis), array.shape[dim])
+    line, have = (array, 1)
+    while have < ways:
+        line = jnp.concatenate(
+            [line, lax.ppermute(line, axis, [(d, (d - have) % ways) for d in range(ways)])],
+            axis=dim,
+        )
+        have = 2 * have
+    return jnp.roll(line, here * hop, axis=dim)
 
 
 def padded_2(x, sides, width):
@@ -145,7 +157,7 @@
     restored = local_transform(filtered, 1.0)
     restored = rotate_by(restored, (jnp.cos(global_angle), jnp.sin(global_angle)))
     shard_piece = (
-        lax.all_gather(restored[0], "range", axis=2, tiled=True),
+        gather_by_bits(restored[0], "range", 2),
         lax.all_gather(restored[1], "range", axis=2, tiled=True),
     )
     shard_count = shard_piece[0].shape[2] // gate_count

time: 395 us -> 371 us (0.939)
  waiting for transfers between devices: 141 us -> 118 us
    ppermute x0 -> x1, waiting for transfers between devices: none -> 40 us  [gather_by_bits(): lax.ppermute(line, axis, [(d, (d - have) % ways) for d in range(ways)])]
    all_gather x1 -> x0, waiting for transfers between devices: 32.5 us -> none  [shards(): lax.all_gather(restored[0], 'range', axis=2, tiled=True)]
    all_gather x1, waiting for transfers between devices: 34.7 us -> 5.36 us  [shards(): lax.all_gather(restored[1], 'range', axis=2, tiled=True)]
    unnamed x12 -> x10, local copies, waits for them, and re-layouts: 48.9 us -> 47.7 us
  transfers between devices with their start and end apart: 6 -> 6, of which waited for: 6 -> 6; matrix products, arithmetic and copies ran while one was open for 3% -> 4% of each run, Pallas kernels for 0% -> 0%
where the time goes in v1:
time: 371 us; the launch traced here: 364 us
  waiting for transfers between devices  118 us (32%)
  local copies, waits for them, and re-layouts  111 us (30%)
  blocking collectives  61.8 us (17%)
  matrix products  24.5 us (7%)
  other arithmetic  24 us (6%)
  between operations  14.2 us (4%)
  starting transfers between devices  10.9 us (3%)
    all_to_all x1, waiting for transfers between devices, shards(): lax.all_to_all(signal, 'chan', split_axis=2, concat_axis=1, tiled=True)  48.2 us
    unnamed x10, local copies, waits for them, and re-layouts  47.7 us
    ppermute x1, waiting for transfers between devices, gather_by_bits(): lax.ppermute(line, axis, [(d, (d - have) % ways) for d in range(ways)])  40 us
    all_to_all x1, blocking collectives, shards(): lax.all_to_all(formed, 'chan', split_axis=1, concat_axis=2, tiled=True)  27.7 us
    all_gather x1, waiting for transfers between devices, shards(): shard_piece = lax.all_gather(beam_data, 'range', axis=3, tiled=True)  20.2 us
    all_to_all x1, blocking collectives, shards(): lax.all_to_all(compressed, 'pulse', split_axis=3, concat_axis=2, tiled=True)  17.2 us
    all_to_all x1, blocking collectives, shards(): lax.all_to_all(mixed_real * mixed_real + mixed_imag * mixed_imag, 'pulse'...  16.9 us
    all_to_all x1, local copies, waits for them, and re-layouts, shards(): lax.all_to_all(compressed, 'pulse', split_axis=3, concat_axis=2, tiled=True)  16 us
  transfers between devices with their start and end apart: 6, of which 6 were waited for; matrix products, arithmetic and copies ran while one was open for 4% of the time, Pallas kernels for 0%

profile of v1, /device:TPU:0, one launch (start us, length us, event | category | flops | bytes accessed | tf_op | source)
XLA Modules:
  0.0 364.5 jit_solution(10016934210120024921)
XLA Ops:
  6.5 4.1 %copy.63 = bf16[2,16,8,4096]{3,1,0,2:T(8,128)(2,1)} copy(bf16[2,16,8,4096]{3,2,1,0:T(8,128)(2,1)} %param.3) | data formatting | bytes 4194304 | tf_op args[0]
  10.6 6.5 %all-to-all-start = ((bf16[2,16,8,4096]{3,1,0,2:T(8,128)(2,1)}), bf16[2,16,8,4096]{3,1,0,2:T(8,128)(2,1)S(1)}, u32[]{:S(2)}, u32[]{:S(2)}) async-start(bf16[2,16,8,4096]{3,1,0,2:T(8,128)(2,1)} %copy.63), calls=%async_computation | async-start | bytes 4194304 | tf_op jit(solution)/shard_map/all_to_all | solution.py:119
  17.1 48.2 %all-to-all-done = bf16[2,16,8,4096]{3,1,0,2:T(8,128)(2,1)S(1)} async-done(((bf16[2,16,8,4096]{3,1,0,2:T(8,128)(2,1)}), bf16[2,16,8,4096]{3,1,0,2:T(8,128)(2,1)S(1)}, u32[]{:S(2)}, u32[]{:S(2)}) %all-to-all-start) | async-done | bytes 2097184 | tf_op jit(solution)/shard_map/all_to_all | solution.py:119
  65.3 2.2 copy.64
  67.5 1.3 copy.98
  70.1 0.9 copy.65
  71.0 27.7 %all_to_all.66 = bf16[2,32,2,4096]{3,2,0,1:T(2,128)(2,1)S(1)} all-to-all(bf16[2,32,2,4096]{3,2,0,1:T(2,128)(2,1)S(1)} %copy.65), channel_id=1, replica_groups=mesh['chan'=4,'pulse'=4,'range'=2] {'chan'}, dimensions={1} | all-to-all | bytes 2097152 | tf_op jit(solution)/shard_map/all_to_all | solution.py:125
  99.3 1.0 copy.67
  100.6 6.4 %reshape.188 = f32[2,4096,2]{2,1,0:T(8,128)} reshape(f32[2,8192]{1,0:T(2,128)S(1)} %copy-done.1) | data formatting | bytes 131072 | tf_op jit(solution)/shard_map/reshape | solution.py:151
  107.0 4.7 %dynamic-slice_reduce_fusion = f32[2,4096]{1,0:T(2,128)S(1)} fusion(f32[2,4096,2]{2,1,0:T(8,128)} %reshape.188, s32[]{:T(128)S(6)} %select_n.146), kind=kLoop, calls=%fused_computation.35 | loop fusion | bytes 65540 | tf_op jit(solution)/shard_map/jit(dynamic_index_in_dim)/dynamic_slice | solution.py:152
  112.5 20.2 %all-gather.3.cloned.1.call-done = bf16[2,8,8,8192]{3,1,2,0:T(8,128)(2,1)} async-done(((bf16[2,8,8,4096]{3,1,2,0:T(8,128)(2,1)}), bf16[2,8,8,8192]{3,1,2,0:T(8,128)(2,1)}) %all-gather.3.cloned.1.call-update) | async-done | bytes 2097168 | tf_op jit(solution)/shard_map/all_gather | solution.py:131
  132.7 3.9 %fusion.278 = (f32[1,8,8,8192]{3,1,2,0:T(8,128)}, f32[1,8,8,8192]{3,1,2,0:T(8,128)}) fusion(bf16[2,8,8,8192]{3,1,2,0:T(8,128)(2,1)} %all-gather.3.cloned.1.call-done), kind=kLoop, calls=%fused_computation.372 | loop fusion | bytes 8388608 | tf_op jit(solution)/shard_map/slice | solution.py:142
  136.7 3.0 reshape.202
  139.7 4.4 %reshape.203 = f32[8,8,2,4096]{3,2,0,1:T(2,128)} reshape(f32[1,8,8,8192]{3,1,2,0:T(8,128)} %get-tuple-element.12) | data formatting | bytes 4194304 | tf_op jit(solution)/shard_map/squeeze | solution.py:142
  144.1 5.8 %subtract_reduce_fusion.1 = (f32[8,8,4096]{2,1,0:T(8,128)S(1)}, f32[8,8,4096]{2,1,0:T(8,128)S(1)}) fusion(f32[8,8,2,4096]{3,2,0,1:T(2,128)} %reshape.203, f32[8,8,2,4096]{3,2,0,1:T(2,128)S(1)} %reshape.202, f32[2]{0:T(128)S(1)} %get-tuple-element.20, f32[2]{0:T(128)S(1)} %get-tuple-element.19), kind=kLoop, calls=%fused_computation.42 | loop fusion | flops 3670016 | bytes 6291472 | tf_op jit(solution)/shard_map/reduce_sum | solution.py:142
  149.8 1.4 fusion.87
  151.3 1.4 fusion.91
  152.7 1.4 fusion.5
  154.1 1.4 fusion.6
  155.6 1.2 fusion.81
  156.8 1.4 fusion.82
  158.2 1.2 convolution_add_fusion.2
  159.4 1.2 convolution_subtract_fusion.2
  160.7 1.2 fusion.83
  161.9 1.2 fusion.84
  163.2 1.2 convolution_add_fusion.1
  164.4 1.2 convolution_subtract_fusion.1
  165.6 1.2 fusion.86
  166.8 1.2 fusion.85
  168.0 2.2 fusion.3
  170.2 2.4 reshape.191
  172.6 2.4 fusion.4
  174.9 1.5 reshape.190
  176.5 1.2 multiply_subtract_fusion
  178.2 40.0 %collective-permute-done = f32[8,8,4096]{2,1,0:T(8,128)} collective-permute-done((f32[8,8,4096]{2,1,0:T(8,128)S(1)}, f32[8,8,4096]{2,1,0:T(8,128)}, u32[]{:S(2)}, u32[]{:S(2)}) %collective-permute-start) | collective-permute-done | bytes 1048608 | tf_op jit(solution)/shard_map/ppermute | solution.py:18
  218.2 1.7 fusion.2
  219.9 5.4 %all-gather.5.cloned.1.call-done = f32[8,8,8192]{2,1,0:T(8,128)} async-done(((f32[8,8,4096]{2,1,0:T(8,128)}), f32[8,8,8192]{2,1,0:T(8,128)}) %all-gather.5.cloned.1.call-update) | async-done | bytes 2097168 | tf_op jit(solution)/shard_map/all_gather | solution.py:161
  225.3 2.5 subtract_reduce_fusion
  228.0 13.8 %copy.80 = bf16[2,8,8,4096]{2,1,0,3:T(8,128)(2,1)} copy(bf16[2,8,8,4096]{3,2,1,0:T(8,128)(2,1)S(1)} %pad_maximum_fusion.2) | data formatting | bytes 2097152 | tf_op jit(solution)/shard_map/stack | solution.py:174
  241.8 20.5 %reshape.205 = bf16[4,2,65536]{2,1,0:T(2,128)(2,1)S(1)} reshape(bf16[4096,2,8,8]{3,2,1,0:T(8,128)(2,1)} %bitcast.154) | data formatting | bytes 2097152
  262.3 17.2 %all_to_all.67 = bf16[4,2,65536]{2,1,0:T(2,128)(2,1)S(1)} all-to-all(bf16[4,2,65536]{2,1,0:T(2,128)(2,1)S(1)} %reshape.205), channel_id=1, replica_groups=mesh['chan'=4,'pulse'=4,'range'=2] {'pulse'}, dimensions={0} | all-to-all | bytes 2097152 | tf_op jit(solution)/shard_map/all_to_all | solution.py:179
  279.5 21.7 %reshape.206 = bf16[4096,2,8,8]{3,2,1,0:T(8,128)(2,1)} reshape(bf16[4,2,65536]{2,1,0:T(2,128)(2,1)S(1)} %all_to_all.67) | data formatting | bytes 2097152
  301.3 16.0 %copy.81 = bf16[2,8,8,4,1024]{4,2,3,1,0:T(8,128)(2,1)S(1)} copy(bf16[2,8,8,4,1024]{2,1,0,4,3:T(8,128)(2,1)} %bitcast.155) | data formatting | bytes 2097152 | tf_op jit(solution)/shard_map/all_to_all | solution.py:179
  319.3 16.9 %all_to_all.68 = f32[8,32,1024]{2,0,1:T(8,128)S(1)} all-to-all(f32[8,32,1024]{2,0,1:T(8,128)S(1)} %copy.82), channel_id=1, replica_groups=mesh['chan'=4,'pulse'=4,'range'=2] {'pulse'}, dimensions={1} | all-to-all | bytes 2097152 | tf_op jit(solution)/shard_map/all_to_all | solution.py:186
  336.9 2.5 collective-permute-start.1
  339.4 1.3 collective-permute-start.2
  340.9 4.2 %collective-permute-done.2 = f32[8,8,20]{2,1,0:T(8,128)S(1)} collective-permute-done((f32[8,8,20]{2,1,0:T(8,128)S(1)}, f32[8,8,20]{2,1,0:T(8,128)S(1)}, u32[]{:S(2)}, u32[]{:S(2)}) %collective-permute-start.2) | collective-permute-done | bytes 5152 | tf_op jit(solution)/shard_map/ppermute | solution.py:33
  345.2 12.0 %fusion.17 = f32[8,8,4096]{2,1,0:T(8,128)} fusion(f32[8,8,4096]{2,1,0:T(8,128)S(1)} %bitcast.173, f32[8,8,20]{2,1,0:T(8,128)S(1)} %collective-permute-done.2, f32[8,8,20]{2,1,0:T(8,128)S(1)} %collective-permute-done.1), kind=kLoop, calls=%fused_computation.67 | loop fusion | flops 17301504 | bytes 2107392 | tf_op jit(solution)/shard_map/div | solution.py:205
  (37 shorter events, 6.6 us)
Async XLA Ops:
  10.6 6.5 %copy-start.2 = (bf16[2,32,64]{2,1,0:T(8,128)(2,1)S(1)}, bf16[2,32,64]{2,1,0:T(8,128)(2,1)}, u32[]{:S(2)}) copy-start(bf16[2,32,64]{2,1,0:T(8,128)(2,1)} %param.4) | copy-start | bytes 24580
  10.6 54.7 %all-to-all-start = ((bf16[2,16,8,4096]{3,1,0,2:T(8,128)(2,1)}), bf16[2,16,8,4096]{3,1,0,2:T(8,128)(2,1)S(1)}, u32[]{:S(2)}, u32[]{:S(2)}) async-start(bf16[2,16,8,4096]{3,1,0,2:T(8,128)(2,1)} %copy.63), calls=%async_computation | async-start | bytes 4194304 | tf_op jit(solution)/shard_map/all_to_all | solution.py:119
  17.1 115.6 %all-gather.3.cloned.1.call-start = ((), (), s32[]{:S(2)}) async-start(), calls=%async_computation.4 | async-start | bytes 3145728 | tf_op jit(solution)/shard_map/all_gather | solution.py:131
  99.3 1.3 copy-start.1
  100.4 124.9 %all-gather.5.cloned.1.call-start = ((), (), s32[]{:S(2)}) async-start(), calls=%async_computation.5 | async-start | bytes 3145728 | tf_op jit(solution)/shard_map/all_gather | solution.py:161
  174.9 1.5 copy-start
  177.8 40.4 %collective-permute-start = (f32[8,8,4096]{2,1,0:T(8,128)S(1)}, f32[8,8,4096]{2,1,0:T(8,128)}, u32[]{:S(2)}, u32[]{:S(2)}) collective-permute-start(f32[8,8,4096]{2,1,0:T(8,128)S(1)} %get-tuple-element.9), channel_id=1, source_target_pairs={{0,1},{1,0},{2,3},{3,2},{4,5},{5,4},{6,7},{7,6},{8,9},{9,8},{10,11... | collective-permute-start | bytes 3145736 | tf_op jit(solution)/shard_map/ppermute | solution.py:18
  336.9 4.0 %collective-permute-start.1 = (f32[8,8,20]{2,1,0:T(8,128)S(1)}, f32[8,8,20]{2,1,0:T(8,128)S(1)}, u32[]{:S(2)}, u32[]{:S(2)}) collective-permute-start(f32[8,8,20]{2,1,0:T(8,128)S(1)} %get-tuple-element.13), channel_id=1, source_target_pairs={{0,1},{2,3},{4,5},{6,7},{8,9},{10,11},{12,13},{14,15},{16,17},{18,... | collective-permute-start | bytes 15368 | tf_op jit(solution)/shard_map/ppermute | solution.py:32
  339.4 5.8 %collective-permute-start.2 = (f32[8,8,20]{2,1,0:T(8,128)S(1)}, f32[8,8,20]{2,1,0:T(8,128)S(1)}, u32[]{:S(2)}, u32[]{:S(2)}) collective-permute-start(f32[8,8,20]{2,1,0:T(8,128)S(1)} %get-tuple-element.14), channel_id=1, source_target_pairs={{1,0},{3,2},{5,4},{7,6},{9,8},{11,10},{13,12},{15,14},{17,16},{19,... | collective-permute-start | bytes 15368 | tf_op jit(solution)/shard_map/ppermute | solution.py:33
Sparse Core Ops, SparseCore 0:
  100.5 32.1 all-gather.2
  177.9 47.3 all-gather.4
